TPU v7x, 32 devices: a whole 2x2x4 slice. The times are simulated.
32 devices in a mesh: dp: 2 (over x), cols: 4 (over z), rows: 4 (over y, core).
Axes of the slice: x: 2, y: 2, z: 4, core: 2. Of those that a mesh axis runs over, the one named last changes fastest.
Arguments:
- h_init: bfloat16 [2, 512, 128, 64], P('dp', 'rows', 'cols'), parts along dimension 0
- c_init: float32 [2, 512, 128, 64], P('dp', 'rows', 'cols'), parts along dimension 0
- w_rec: bfloat16 [3, 3, 64, 256], replicated
- gate_bias: float32 [32, 256], replicated
Outputs:
- output 1: bfloat16 [32, 2, 512, 128, 64], P(None, 'dp', 'rows', 'cols'), parts along dimension 1
- output 2: float32 [2, 512, 128, 64], P('dp', 'rows', 'cols'), parts along dimension 0
There are 2 independent parts. A program takes and returns all parts, laid end to end along the dimension named above; an argument that names none is the same for every part.
All inputs are finite; a program needn't handle non-finite values.
Results may differ from a plain program's by a relative error of at most 0.00444045.
Values are sent between devices in bfloat16 or wider.
A program may use at most 1 GiB of HBM per device.

v0:
```python
import jax
import jax.numpy as jnp
from jax import lax
from jax.sharding import PartitionSpec as P


def lstm_update(gate_pre, c_prev):
    in_gate, forget_gate, out_gate, cand_gate = jnp.split(gate_pre, 4, axis=-1)
    c_next = jax.nn.sigmoid(forget_gate) * c_prev + jax.nn.sigmoid(in_gate) * jnp.tanh(cand_gate)
    h_next = (jax.nn.sigmoid(out_gate) * jnp.tanh(c_next)).astype(jnp.bfloat16)
    return h_next, c_next


def solution(mesh):
    row_count = mesh.shape["rows"]
    col_count = mesh.shape["cols"]
    rows_down = [(src_pos, src_pos + 1) for src_pos in range(row_count - 1)]
    rows_up = [(src_pos + 1, src_pos) for src_pos in range(row_count - 1)]
    cols_right = [(src_pos, src_pos + 1) for src_pos in range(col_count - 1)]
    cols_left = [(src_pos + 1, src_pos) for src_pos in range(col_count - 1)]

    def with_halo(tile):
        from_above = lax.ppermute(tile[:, -1:], "rows", rows_down)
        from_below = lax.ppermute(tile[:, :1], "rows", rows_up)
        tall_tile = jnp.concatenate([from_above, tile, from_below], axis=1)
        from_left = lax.ppermute(tall_tile[:, :, -1:], "cols", cols_right)
        from_right = lax.ppermute(tall_tile[:, :, :1], "cols", cols_left)
        return jnp.concatenate([from_left, tall_tile, from_right], axis=2)

    def device_fn(h_init, c_init, w_rec, gate_bias):
        def one_step(carry_in, bias_row):
            h_prev, c_prev = carry_in
            padded = with_halo(h_prev)
            gate_pre = lax.conv_general_dilated(padded, w_rec, (1, 1), "VALID", dimension_numbers=("NHWC", "HWIO", "NHWC"), preferred_element_type=jnp.float32) + bias_row
            h_next, c_next = lstm_update(gate_pre, c_prev)
            return (h_next, c_next), h_next

        final_state, h_seq = lax.scan(one_step, (h_init, c_init), gate_bias)
        return h_seq, final_state[1]

    state_spec = P("dp", "rows", "cols", None)
    return jax.shard_map(device_fn, mesh=mesh, in_specs=(state_spec, state_spec, P(), P()), out_specs=(P(None, "dp", "rows", "cols", None), state_spec), check_vma=False)
```

profile of v0, /device:TPU:0, one launch (start us, length us, event | category | flops | bytes accessed | tf_op | source)
XLA Modules:
  0.0 1307.8 jit_solution(16688038700838345801)
XLA Ops:
  3.1 1304.8 %while.14 = (s32[]{:T(128)}, bf16[1,128,32,64]{1,3,2,0:T(8,128)(2,1)S(1)}, f32[1,128,32,64]{1,3,2,0:T(8,128)}, bf16[32,1,128,32,64]{2,4,3,1,0:T(8,128)(2,1)}, bf...) while((s32[]{:T(128)}, ...), condition=%wide.region_1.2_spmd, body=%wide.region_0.1_spmd.sunk | while | flops 1522620416 | bytes 56174444 | solution.py:38
  39.8 7.6 collective-permute-start.1
  78.5 10.2 collective-permute-start.1
  119.8 9.9 collective-permute-start.1
  160.8 9.9 collective-permute-start.1
  201.8 9.9 collective-permute-start.1
  242.9 9.9 collective-permute-start.1
  283.9 9.9 collective-permute-start.1
  324.9 9.9 collective-permute-start.1
  365.9 9.9 collective-permute-start.1
  406.9 9.9 collective-permute-start.1
  447.9 9.9 collective-permute-start.1
  489.0 9.9 collective-permute-start.1
  530.0 9.9 collective-permute-start.1
  571.0 9.9 collective-permute-start.1
  612.0 9.9 collective-permute-start.1
  653.1 9.9 collective-permute-start.1
  694.1 9.9 collective-permute-start.1
  735.1 9.9 collective-permute-start.1
  776.1 9.9 collective-permute-start.1
  817.1 9.9 collective-permute-start.1
  858.1 9.9 collective-permute-start.1
  899.2 9.9 collective-permute-start.1
  940.2 9.9 collective-permute-start.1
  981.2 9.9 collective-permute-start.1
  1022.2 9.9 collective-permute-start.1
  1063.2 9.9 collective-permute-start.1
  1104.2 9.9 collective-permute-start.1
  1145.3 9.9 collective-permute-start.1
  1186.3 9.9 collective-permute-start.1
  1227.3 9.9 collective-permute-start.1
  1268.3 9.9 collective-permute-start.1
  (745 shorter events, 998.1 us)
Async XLA Ops:
  77.2 11.5 collective-permute-start
  78.5 11.7 collective-permute-start.1
  119.8 11.4 collective-permute-start.1
  160.8 11.4 collective-permute-start.1
  201.8 11.4 collective-permute-start.1
  241.6 11.2 collective-permute-start
  242.9 11.4 collective-permute-start.1
  283.9 11.4 collective-permute-start.1
  324.9 11.4 collective-permute-start.1
  365.9 11.4 collective-permute-start.1
  406.9 11.4 collective-permute-start.1
  447.9 11.4 collective-permute-start.1
  489.0 11.4 collective-permute-start.1
  530.0 11.4 collective-permute-start.1
  571.0 11.4 collective-permute-start.1
  612.0 11.4 collective-permute-start.1
  653.1 11.4 collective-permute-start.1
  694.1 11.4 collective-permute-start.1
  735.1 11.4 collective-permute-start.1
  776.1 11.4 collective-permute-start.1
  817.1 11.4 collective-permute-start.1
  858.1 11.4 collective-permute-start.1
  899.2 11.4 collective-permute-start.1
  940.2 11.4 collective-permute-start.1
  981.2 11.4 collective-permute-start.1
  1022.2 11.4 collective-permute-start.1
  1063.2 11.4 collective-permute-start.1
  1104.2 11.4 collective-permute-start.1
  1145.3 11.4 collective-permute-start.1
  1186.3 11.4 collective-permute-start.1
  1227.3 11.4 collective-permute-start.1
  1268.3 11.4 collective-permute-start.1
  (163 other events, 828.4 us)
where the time goes:
time: 1330 us; the launch traced here: 1310 us
  starting transfers between devices  538 us (40%)
  local copies, waits for them, and re-layouts  334 us (25%)
  other arithmetic  210 us (16%)
  matrix products  146 us (11%)
  waiting for transfers between devices  75.1 us (6%)
    ppermute x32, starting transfers between devices, with_halo(): from_above = lax.ppermute(tile[:, -1:], 'rows', rows_down)  309 us
    conv_general_dilated x96, local copies, waits for them, and re-layouts, one_step(): lax.conv_general_dilated(padded, w_rec, (1, 1), 'VALID', dimension_number...  262 us
    ppermute x32, starting transfers between devices, with_halo(): from_left = lax.ppermute(tall_tile[:, :, -1:], 'cols', cols_right)  147 us
    conv_general_dilated x32, matrix products, one_step(): lax.conv_general_dilated(padded, w_rec, (1, 1), 'VALID', dimension_number...  146 us
    add x32, other arithmetic, one_step(): lax.conv_general_dilated(padded, w_rec, (1, 1), 'VALID', dimension_number...  103 us
    ppermute x32, waiting for transfers between devices, with_halo(): from_above = lax.ppermute(tile[:, -1:], 'rows', rows_down)  47.2 us
    dynamic_update_slice x32, other arithmetic, device_fn(): final_state, h_seq = lax.scan(one_step, (h_init, c_init), gate_bias)  44.9 us
    ppermute x32, starting transfers between devices, with_halo(): from_below = lax.ppermute(tile[:, :1], 'rows', rows_up)  41.3 us
  transfers between devices with their start and end apart: 128, of which 64 were waited for; matrix products, arithmetic and copies ran while one was open for 2% of the time, Pallas kernels for 0%

commit v1 on v0

v1 whole, which is shorter than its diff:
```python
import functools

import jax
import jax.numpy as jnp
from jax import lax
from jax.experimental import pallas as pl
from jax.experimental.pallas import tpu as pltpu
from jax.sharding import PartitionSpec as P

UP, DOWN, LEFT, RIGHT, UP_LEFT, UP_RIGHT, DOWN_LEFT, DOWN_RIGHT = range(8)
OFFSETS = ((-1, 0), (1, 0), (0, -1), (0, 1), (-1, -1), (-1, 1), (1, -1), (1, 1))
OPPOSITE = (DOWN, UP, RIGHT, LEFT, DOWN_RIGHT, DOWN_LEFT, UP_RIGHT, UP_LEFT)
EDGE_DIRS = (UP, DOWN, UP_LEFT, UP_RIGHT, DOWN_LEFT, DOWN_RIGHT)
MESH = pl.DeviceIdType.MESH


def kernel(steps, tiles, chunks, rows_n, cols_n, h_init, c_init, w_ref, bias_ref, h_seq, c_last,
           hl0, hr0, hl1, hr1, cs, bs, ghost, pack_e, pack_c, recv_e, recv_c,
           init_sem, out_sem, send_col, recv_col, send_e, recv_e_sem, send_c, recv_c_sem):
    ch, lanes = h_init.shape[1], h_init.shape[2]
    cols = 2 * tiles
    groups = ch // 16
    stacks = ((hl0, hr0), (hl1, hr1))
    row, col = lax.axis_index("rows"), lax.axis_index("cols")
    chunk_of = {j: (k, j - chunk[0]) for k, chunk in enumerate(chunks) for j in chunk}

    has, target, slot = [], [], []
    for d, (dr, dc) in enumerate(OFFSETS):
        r, c = row + dr, col + dc
        has.append((r >= 0) & (r < rows_n) & (c >= 0) & (c < cols_n))
        target.append({"rows": r, "cols": c})
        slot.append(OPPOSITE[d])

    def at(d, action):
        pl.when(has[d])(action)

    for ref in (ghost, recv_e, recv_c):
        ref[...] = jnp.zeros_like(ref)
    barrier = pltpu.get_barrier_semaphore()
    for d in range(8):
        at(d, lambda d=d: pl.semaphore_signal(barrier, inc=1, device_id=target[d], device_id_type=MESH))
    around_r = 1 + has[UP].astype(jnp.int32) + has[DOWN].astype(jnp.int32)
    around_c = 1 + has[LEFT].astype(jnp.int32) + has[RIGHT].astype(jnp.int32)
    pl.semaphore_wait(barrier, around_r * around_c - 1)

    def column(side, j):
        return j if side == 0 else cols - 1 - j

    loads = []
    for side in range(2):
        for j in range(tiles):
            loads.append(pltpu.make_async_copy(h_init.at[column(side, j)], stacks[0][side].at[j + 1, pl.ds(ch, ch)], init_sem.at[0, side, j]))
            loads.append(pltpu.make_async_copy(c_init.at[column(side, j)], cs.at[side, j], init_sem.at[1, side, j]))
    for copy in loads:
        copy.start()
    for copy in loads:
        copy.wait()

    lane = lax.broadcasted_iota(jnp.int16, (16, lanes), 1)
    pair_of = lax.shift_right_logical(lane, jnp.int16(1))
    even = (lane & jnp.int16(1)) == jnp.int16(0)
    first, last = lane == jnp.int16(0), lane == jnp.int16(lanes - 1)
    zero = jnp.zeros((16, lanes), jnp.bfloat16)

    def pack(packed, local, side, h):
        for g in range(groups):
            pair = 16 * g + 2 * local + side
            moved = pltpu.roll(h[16 * g:16 * g + 16], (1 + 2 * pair) % lanes, 1)
            packed = jnp.where(pair_of == jnp.int16(pair), moved, packed)
        return packed

    def col_copy(p, d):
        side = d - LEFT
        return pltpu.make_async_remote_copy(
            src_ref=stacks[p][side].at[1, pl.ds(ch, ch)], dst_ref=ghost.at[p, slot[d] - LEFT],
            send_sem=send_col.at[p, side], recv_sem=recv_col.at[p, slot[d] - LEFT], device_id=target[d], device_id_type=MESH)

    def col_wait(p, side):
        pltpu.make_async_copy(ghost.at[p, side], ghost.at[p, side], recv_col.at[p, side]).wait()

    def edge_copy(p, d):
        return pltpu.make_async_remote_copy(
            src_ref=pack_e.at[p], dst_ref=recv_e.at[p, slot[d]],
            send_sem=send_e.at[p, d], recv_sem=recv_e_sem.at[p, slot[d]], device_id=target[d], device_id_type=MESH)

    def edge_wait(p, d):
        pltpu.make_async_copy(recv_e.at[p, d], recv_e.at[p, d], recv_e_sem.at[p, d]).wait()

    def chunk_copy(p, k, d):
        return pltpu.make_async_remote_copy(
            src_ref=pack_c.at[p, k - 1], dst_ref=recv_c.at[p, k - 1, slot[d]],
            send_sem=send_c.at[p, k - 1, d], recv_sem=recv_c_sem.at[p, k - 1, slot[d]], device_id=target[d], device_id_type=MESH)

    def chunk_wait(p, k, d):
        pltpu.make_async_copy(recv_c.at[p, k - 1, d], recv_c.at[p, k - 1, d], recv_c_sem.at[p, k - 1, d]).wait()

    def send_cols(p):
        for d in (LEFT, RIGHT):
            at(d, lambda d=d: col_copy(p, d).start())

    def send_chunk(p, k):
        if k == 0:
            for d in EDGE_DIRS:
                at(d, lambda d=d: edge_copy(p, d).start())
        else:
            for d in (UP, DOWN):
                at(d, lambda d=d: chunk_copy(p, k, d).start())

    def wait_sends(p):
        for d in range(8):
            def wait_for(d=d):
                if d in (LEFT, RIGHT):
                    col_copy(p, d).wait_send()
                else:
                    edge_copy(p, d).wait_send()
                if d in (UP, DOWN):
                    for k in range(1, len(chunks)):
                        chunk_copy(p, k, d).wait_send()

            at(d, wait_for)

    def wait_recv(p, k):
        if k == 0:
            for d in (LEFT, RIGHT):
                at(d, lambda d=d: col_wait(p, d - LEFT))
            for d in EDGE_DIRS:
                at(d, lambda d=d: edge_wait(p, d))
        else:
            for d in (UP, DOWN):
                at(d, lambda d=d: chunk_wait(p, k, d))

    def halo(above, below):
        return jnp.where(even, above, below)

    def shifted(dst, s, h, edges, pair0):
        for g in range(groups):
            part = h[16 * g:16 * g + 16]
            edge = pltpu.roll(edges, (-(2 * (16 * g + pair0) + 1)) % lanes, 1)
            dst[s, pl.ds(16 * g, 16)] = pltpu.roll(jnp.where(last, edge, part), 1, 1)
            dst[s, pl.ds(2 * ch + 16 * g, 16)] = pltpu.roll(jnp.where(first, edge, part), lanes - 1, 1)

    def prepare_ghosts(p):
        for side, (up, down) in enumerate(((UP_LEFT, DOWN_LEFT), (UP_RIGHT, DOWN_RIGHT))):
            h = ghost[p, side]
            dst = stacks[p][side]
            dst[0, pl.ds(ch, ch)] = h
            shifted(dst, 0, h, halo(recv_e[p, up], recv_e[p, down]), 1 - side)

    def prepare(p, k):
        if k == 0:
            prepare_ghosts(p)
            edges = halo(recv_e[p, UP], recv_e[p, DOWN])
        else:
            edges = halo(recv_c[p, k - 1, UP], recv_c[p, k - 1, DOWN])
        for local, j in enumerate(chunks[k]):
            for side in range(2):
                dst = stacks[p][side]
                shifted(dst, j + 1, dst[j + 1, pl.ds(ch, ch)], edges, 2 * local + side)

    def matmul(p, j):
        left, right = stacks[p]
        flat = lambda ref, s: ref[s]
        l_next = flat(left, j + 2) if j + 1 < tiles else flat(right, tiles)
        r_next = flat(right, j + 2) if j + 1 < tiles else flat(left, tiles)
        stack_l = jnp.concatenate([flat(left, j), flat(left, j + 1), l_next], axis=0)
        stack_r = jnp.concatenate([r_next, flat(right, j + 1), flat(right, j)], axis=0)
        stack = jnp.concatenate([stack_l, stack_r], axis=1)
        return jnp.dot(w_ref[...], stack, preferred_element_type=jnp.float32)

    def update(side, j, gates):
        part = gates[:, side * lanes:(side + 1) * lanes] + bs[...]
        in_t, forget_t, out_t, cand = (part[ch * b:ch * b + ch] for b in range(4))
        c = (0.5 * jnp.tanh(forget_t) + 0.5) * cs[side, j] + (0.5 * jnp.tanh(in_t) + 0.5) * jnp.tanh(cand)
        cs[side, j] = c
        return ((0.5 * jnp.tanh(out_t) + 0.5) * jnp.tanh(c)).astype(jnp.bfloat16)

    def out_copy(p, t, side, j):
        return pltpu.make_async_copy(stacks[p][side].at[j + 1, pl.ds(ch, ch)], h_seq.at[t, column(side, j)], out_sem.at[p, side, j])

    def wait_outs(p):
        for side in range(2):
            for j in range(tiles):
                out_copy(p, 0, side, j).wait()

    def store_pack(p, k, packed):
        if k == 0:
            pack_e[p] = packed
        else:
            pack_c[p, k - 1] = packed

    def step(t, p):
        q = 1 - p
        line = bias_ref[pl.ds(t, 1), :]
        bs[...] = jnp.transpose(jnp.broadcast_to(line, (lanes, line.shape[1])))
        for k in range(2):
            wait_recv(p, k)
            prepare(p, k)
        ready = 1
        packed = zero
        for j in range(tiles):
            if j + 1 < tiles and chunk_of[j + 1][0] > ready:
                ready = chunk_of[j + 1][0]
                wait_recv(p, ready)
                prepare(p, ready)
            gates = matmul(p, j)
            k, local = chunk_of[j]
            for side in range(2):
                h = update(side, j, gates)
                stacks[q][side][j + 1, pl.ds(ch, ch)] = h
                packed = pack(packed, local, side, h)
            for side in range(2):
                out_copy(q, t, side, j).start()
            if j == 0:
                send_cols(q)
            if j == chunks[k][-1]:
                store_pack(q, k, packed)
                packed = zero
                send_chunk(q, k)
        wait_sends(p)

    for k, chunk in enumerate(chunks):
        packed = zero
        for local, j in enumerate(chunk):
            for side in range(2):
                packed = pack(packed, local, side, stacks[0][side][j + 1, pl.ds(ch, ch)])
        store_pack(0, k, packed)
        if k == 0:
            send_cols(0)
        send_chunk(0, k)

    def two_steps(i, carry):
        step(2 * i, 0)

        @pl.when(i > 0)
        def _():
            wait_outs(0)

        step(2 * i + 1, 1)
        wait_outs(1)
        return carry

    lax.fori_loop(0, steps // 2, two_steps, 0)
    for k in range(len(chunks)):
        wait_recv(0, k)
    wait_sends(0)
    wait_outs(0)
    stores = [pltpu.make_async_copy(cs.at[side, j], c_last.at[column(side, j)], init_sem.at[1, side, j]) for side in range(2) for j in range(tiles)]
    for copy in stores:
        copy.start()
    for copy in stores:
        copy.wait()


def solution(mesh):
    rows_n, cols_n = mesh.shape["rows"], mesh.shape["cols"]

    def device_fn(h_init, c_init, w_rec, gate_bias):
        _, height, width, ch = h_init.shape
        steps, gates_n = gate_bias.shape
        tiles = width // 2
        chunks = (tuple(range(1)), tuple(range(1, 6)), tuple(range(6, 11)), tuple(range(11, tiles)))
        scale = jnp.where(jnp.arange(gates_n) < 3 * ch, 0.5, 1.0).astype(jnp.float32)
        w = (jnp.transpose(w_rec, (3, 1, 0, 2)).reshape(gates_n, 9 * ch).astype(jnp.float32) * scale[:, None]).astype(jnp.bfloat16)
        bias = gate_bias * scale
        h_in = jnp.transpose(h_init[0], (1, 2, 0))
        c_in = jnp.transpose(c_init[0], (1, 2, 0))
        stack = pltpu.VMEM((tiles + 1, 3 * ch, height), jnp.bfloat16)
        any_spec = pl.BlockSpec(memory_space=pl.ANY)
        vmem_spec = pl.BlockSpec(memory_space=pltpu.VMEM)
        dma = pltpu.SemaphoreType.DMA
        h_seq, c_last = pl.pallas_call(
            functools.partial(kernel, steps, tiles, chunks, rows_n, cols_n),
            out_shape=(jax.ShapeDtypeStruct((steps, width, ch, height), jnp.bfloat16),
                       jax.ShapeDtypeStruct((width, ch, height), jnp.float32)),
            in_specs=[any_spec, any_spec, vmem_spec, vmem_spec],
            out_specs=(any_spec, any_spec),
            scratch_shapes=[
                stack, stack, stack, stack,
                pltpu.VMEM((2, tiles, ch, height), jnp.float32),
                pltpu.VMEM((gates_n, height), jnp.float32),
                pltpu.VMEM((2, 2, ch, height), jnp.bfloat16),
                pltpu.VMEM((2, 16, height), jnp.bfloat16),
                pltpu.VMEM((2, len(chunks) - 1, 16, height), jnp.bfloat16),
                pltpu.VMEM((2, 8, 16, height), jnp.bfloat16),
                pltpu.VMEM((2, len(chunks) - 1, 2, 16, height), jnp.bfloat16),
                dma((2, 2, tiles)), dma((2, 2, tiles)),
                dma((2, 2)), dma((2, 2)), dma((2, 8)), dma((2, 8)),
                dma((2, len(chunks) - 1, 2)), dma((2, len(chunks) - 1, 2)),
            ],
            compiler_params=pltpu.CompilerParams(collective_id=0, has_side_effects=True, vmem_limit_bytes=60 * 1024 * 1024),
        )(h_in, c_in, w, bias)
        return jnp.transpose(h_seq, (0, 3, 1, 2))[:, None], jnp.transpose(c_last, (2, 0, 1))[None]

    state_spec = P("dp", "rows", "cols", None)
    return jax.shard_map(device_fn, mesh=mesh, in_specs=(state_spec, state_spec, P(), P()), out_specs=(P(None, "dp", "rows", "cols", None), state_spec), check_vma=False)
```

time: 1330 us -> 174 us (0.13); the launches traced: 1310 us -> 172 us
  starting transfers between devices: 538 us -> 0 us
  local copies, waits for them, and re-layouts: 334 us -> 15.2 us
  other arithmetic: 210 us -> 3.22 us
  Pallas kernels: 0 us -> 153 us
  matrix products: 146 us -> 0 us
  waiting for transfers between devices: 75.1 us -> 0 us
    ppermute x128 -> x0, starting transfers between devices: 538 us -> none  [the longest x32 309 us: with_halo(): from_above = lax.ppermute(tile[:, -1:], 'rows', rows_down)]
    conv_general_dilated x96 -> x0, local copies, waits for them, and re-layouts: 262 us -> none  [one_step(): lax.conv_general_dilated(padded, w_rec, (1, 1), 'VALID', dimension_number...]
    pallas_call x0 -> x1, Pallas kernels: none -> 153 us  [device_fn(): pl.pallas_call(functools.partial(kernel, steps, tiles, chunks, rows_n, co...]
    conv_general_dilated x32 -> x0, matrix products: 146 us -> none  [one_step(): lax.conv_general_dilated(padded, w_rec, (1, 1), 'VALID', dimension_number...]
    add x32 -> x0, other arithmetic: 103 us -> none  [one_step(): lax.conv_general_dilated(padded, w_rec, (1, 1), 'VALID', dimension_number...]
    ppermute x128 -> x0, waiting for transfers between devices: 75.1 us -> none  [the longest x32 47.2 us: with_halo(): from_above = lax.ppermute(tile[:, -1:], 'rows', rows_down)]
    dynamic_update_slice x32 -> x0, other arithmetic: 44.9 us -> none  [device_fn(): final_state, h_seq = lax.scan(one_step, (h_init, c_init), gate_bias)]
    div x32 -> x0, other arithmetic: 38.2 us -> none  [lstm_update(): jax.nn.sigmoid(forget_gate) * c_prev]
  transfers between devices with their start and end apart: 128 -> 0, of which waited for: 64 -> 0; matrix products, arithmetic and copies ran while one was open for 2% -> 0% of each run, Pallas kernels for 0% -> 0%
where the time goes in v1:
time: 174 us; the launch traced here: 172 us
  Pallas kernels  153 us (88%)
  local copies, waits for them, and re-layouts  15.2 us (9%)
  other arithmetic  3.22 us (2%)
    pallas_call x1, Pallas kernels, device_fn(): pl.pallas_call(functools.partial(kernel, steps, tiles, chunks, rows_n, co...  153 us
    unnamed x4, local copies, waits for them, and re-layouts  15 us

profile of v1, /device:TPU:0, one launch (start us, length us, event | category | flops | bytes accessed | tf_op | source)
XLA Modules:
  0.0 172.5 jit_solution(16344715534177214633)
XLA Ops:
  0.6 1.4 broadcast_multiply_fusion.bias_ref
  2.0 1.0 copy_convert_fusion
  3.0 0.2 copy.12
  3.3 0.8 multiply_convert_fusion.w_ref
  4.1 153.4 %shard_map.59 = (bf16[32,32,64,128]{3,2,1,0:T(8,128)(2,1)}, f32[32,64,128]{2,1,0:T(8,128)}) custom-call(bf16[32,64,128]{2,1,0:T(8,128)(2,1)} %bitcast.21, f32[32,64,128]{2,1,0:T(8,128)} %bitcast.20, bf16[256,576]{1,0:T(8,128)(2,1)} %multiply_convert_fusion.w_ref, f32[32,256]{1,0:T(8,128)} %broadcast_multiply_fusion.bias_ref), custom_call_target="tpu_custom_call" | custom-call | tf_op jit(solution)/shard_map/pallas_call | solution.py:271
  157.5 0.0 copy-start
  157.5 14.0 %copy.18 = bf16[32,1,128,32,64]{2,4,3,1,0:T(8,128)(2,1)} copy(bf16[32,1,128,32,64]{2,4,3,1,0:T(8,128)(2,1)} %bitcast.17) | data formatting | bytes 33554432
  171.5 0.0 copy-done
  171.5 1.0 copy.19
  (1 shorter events, 0.0 us)
Async XLA Ops:
  157.5 14.0 %copy-start = (f32[32,64,128]{2,1,0:T(8,128)S(1)}, f32[32,64,128]{2,1,0:T(8,128)}, u32[]{:S(2)}) copy-start(f32[32,64,128]{2,1,0:T(8,128)} %get-tuple-element.5) | copy-start | bytes 3145732

commit v2 on v1

--- a/solution.py
+++ b/solution.py
@@ -15,7 +15,7 @@
 
 
 def kernel(steps, tiles, chunks, rows_n, cols_n, h_init, c_init, w_ref, bias_ref, h_seq, c_last,
-           hl0, hr0, hl1, hr1, cs, bs, ghost, pack_e, pack_c, recv_e, recv_c,
+           hl0, hr0, hl1, hr1, cs, ws, bs, ghost, pack_e, pack_c, recv_e, recv_c,
            init_sem, out_sem, send_col, recv_col, send_e, recv_e_sem, send_c, recv_c_sem):
     ch, lanes = h_init.shape[1], h_init.shape[2]
     cols = 2 * tiles
@@ -56,6 +56,9 @@
     for copy in loads:
         copy.wait()
 
+    ws[pl.ds(0, 3 * ch), :] = w_ref[pl.ds(0, 3 * ch), :] * jnp.bfloat16(0.5)
+    ws[pl.ds(3 * ch, ch), :] = w_ref[pl.ds(3 * ch, ch), :]
+    scale = jnp.where(lax.broadcasted_iota(jnp.int32, (1, 4 * ch), 1) < 3 * ch, 0.5, 1.0).astype(jnp.float32)
     lane = lax.broadcasted_iota(jnp.int16, (16, lanes), 1)
     pair_of = lax.shift_right_logical(lane, jnp.int16(1))
     even = (lane & jnp.int16(1)) == jnp.int16(0)
@@ -165,7 +168,7 @@
         stack_l = jnp.concatenate([flat(left, j), flat(left, j + 1), l_next], axis=0)
         stack_r = jnp.concatenate([r_next, flat(right, j + 1), flat(right, j)], axis=0)
         stack = jnp.concatenate([stack_l, stack_r], axis=1)
-        return jnp.dot(w_ref[...], stack, preferred_element_type=jnp.float32)
+        return jnp.dot(ws[...], stack, preferred_element_type=jnp.float32)
 
     def update(side, j, gates):
         part = gates[:, side * lanes:(side + 1) * lanes] + bs[...]
@@ -190,7 +193,7 @@
 
     def step(t, p):
         q = 1 - p
-        line = bias_ref[pl.ds(t, 1), :]
+        line = bias_ref[pl.ds(t, 1), :] * scale
         bs[...] = jnp.transpose(jnp.broadcast_to(line, (lanes, line.shape[1])))
         for k in range(2):
             wait_recv(p, k)
@@ -258,10 +261,8 @@
         _, height, width, ch = h_init.shape
         steps, gates_n = gate_bias.shape
         tiles = width // 2
-        chunks = (tuple(range(1)), tuple(range(1, 6)), tuple(range(6, 11)), tuple(range(11, tiles)))
-        scale = jnp.where(jnp.arange(gates_n) < 3 * ch, 0.5, 1.0).astype(jnp.float32)
-        w = (jnp.transpose(w_rec, (3, 1, 0, 2)).reshape(gates_n, 9 * ch).astype(jnp.float32) * scale[:, None]).astype(jnp.bfloat16)
-        bias = gate_bias * scale
+        chunks = (tuple(range(1)), tuple(range(1, tiles // 2)), tuple(range(tiles // 2, tiles)))
+        w = jnp.transpose(w_rec, (3, 1, 0, 2)).reshape(gates_n, 9 * ch)
         h_in = jnp.transpose(h_init[0], (1, 2, 0))
         c_in = jnp.transpose(c_init[0], (1, 2, 0))
         stack = pltpu.VMEM((tiles + 1, 3 * ch, height), jnp.bfloat16)
@@ -277,6 +278,7 @@
             scratch_shapes=[
                 stack, stack, stack, stack,
                 pltpu.VMEM((2, tiles, ch, height), jnp.float32),
+                pltpu.VMEM((gates_n, 9 * ch), jnp.bfloat16),
                 pltpu.VMEM((gates_n, height), jnp.float32),
                 pltpu.VMEM((2, 2, ch, height), jnp.bfloat16),
                 pltpu.VMEM((2, 16, height), jnp.bfloat16),
@@ -288,7 +290,7 @@
                 dma((2, len(chunks) - 1, 2)), dma((2, len(chunks) - 1, 2)),
             ],
             compiler_params=pltpu.CompilerParams(collective_id=0, has_side_effects=True, vmem_limit_bytes=60 * 1024 * 1024),
-        )(h_in, c_in, w, bias)
+        )(h_in, c_in, w, gate_bias)
         return jnp.transpose(h_seq, (0, 3, 1, 2))[:, None], jnp.transpose(c_last, (2, 0, 1))[None]
 
     state_spec = P("dp", "rows", "cols", None)

time: 174 us -> 167 us (0.960)
  Pallas kernels: 153 us -> 148 us
  other arithmetic: 3.22 us -> 0 us
    pallas_call x1, Pallas kernels: 153 us -> 148 us  [device_fn(): pl.pallas_call(functools.partial(kernel, steps, tiles, chunks, rows_n, co...]
    convert_element_type x2 -> x0, other arithmetic: 1.83 us -> none  [the longest x1 1 us: device_fn(): jnp.transpose(w_rec, (3, 1, 0, 2)).reshape(gates_n, 9 * ch)]
    unnamed x4 -> x5, local copies, waits for them, and re-layouts: 15 us -> 16 us
where the time goes in v2:
time: 167 us; the launch traced here: 166 us
  Pallas kernels  148 us (89%)
  local copies, waits for them, and re-layouts  16.9 us (10%)
    pallas_call x1, Pallas kernels, device_fn(): pl.pallas_call(functools.partial(kernel, steps, tiles, chunks, rows_n, co...  148 us
    unnamed x5, local copies, waits for them, and re-layouts  16 us

profile of v2, /device:TPU:0, one launch (start us, length us, event | category | flops | bytes accessed | tf_op | source)
XLA Modules:
  0.0 165.7 jit_solution(15522128756912029190)
XLA Ops:
  0.6 1.0 copy.8
  1.6 0.9 copy.9.w_ref
  2.5 148.2 %shard_map.59 = (bf16[32,32,64,128]{3,2,1,0:T(8,128)(2,1)}, f32[32,64,128]{2,1,0:T(8,128)}) custom-call(bf16[32,64,128]{2,1,0:T(8,128)(2,1)} %bitcast.21, f32[32,64,128]{2,1,0:T(8,128)} %bitcast.20, bf16[256,576]{1,0:T(8,128)(2,1)} %copy.9.w_ref, f32[32,256]{1,0:T(8,128)} %bias_ref.1), custom_call_target="tpu_custom_call" | custom-call | tf_op jit(solution)/shard_map/pallas_call | solution.py:272
  150.7 0.0 copy-start
  150.7 14.0 %copy.13 = bf16[32,1,128,32,64]{2,4,3,1,0:T(8,128)(2,1)} copy(bf16[32,1,128,32,64]{2,4,3,1,0:T(8,128)(2,1)} %bitcast.17) | data formatting | bytes 33554432
  164.7 0.0 copy-done
  164.7 1.0 copy.14
Async XLA Ops:
  150.7 14.0 %copy-start = (f32[32,64,128]{2,1,0:T(8,128)S(1)}, f32[32,64,128]{2,1,0:T(8,128)}, u32[]{:S(2)}) copy-start(f32[32,64,128]{2,1,0:T(8,128)} %get-tuple-element.5) | copy-start | bytes 3145732

commit v3 on v2

--- a/solution.py
+++ b/solution.py
@@ -31,8 +31,8 @@
         target.append({"rows": r, "cols": c})
         slot.append(OPPOSITE[d])
 
-    def at(d, action):
-        pl.when(has[d])(action)
+    def at(d, action, live=None):
+        pl.when(has[d] if live is None else has[d] & live)(action)
 
     for ref in (ghost, recv_e, recv_c):
         ref[...] = jnp.zeros_like(ref)
@@ -97,17 +97,17 @@
     def chunk_wait(p, k, d):
         pltpu.make_async_copy(recv_c.at[p, k - 1, d], recv_c.at[p, k - 1, d], recv_c_sem.at[p, k - 1, d]).wait()
 
-    def send_cols(p):
+    def send_cols(p, live=None):
         for d in (LEFT, RIGHT):
-            at(d, lambda d=d: col_copy(p, d).start())
-
-    def send_chunk(p, k):
+            at(d, lambda d=d: col_copy(p, d).start(), live)
+
+    def send_chunk(p, k, live=None):
         if k == 0:
             for d in EDGE_DIRS:
-                at(d, lambda d=d: edge_copy(p, d).start())
+                at(d, lambda d=d: edge_copy(p, d).start(), live)
         else:
             for d in (UP, DOWN):
-                at(d, lambda d=d: chunk_copy(p, k, d).start())
+                at(d, lambda d=d: chunk_copy(p, k, d).start(), live)
 
     def wait_sends(p):
         for d in range(8):
@@ -193,6 +193,7 @@
 
     def step(t, p):
         q = 1 - p
+        live = t < steps - 1 if p else None
         line = bias_ref[pl.ds(t, 1), :] * scale
         bs[...] = jnp.transpose(jnp.broadcast_to(line, (lanes, line.shape[1])))
         for k in range(2):
@@ -214,11 +215,11 @@
             for side in range(2):
                 out_copy(q, t, side, j).start()
             if j == 0:
-                send_cols(q)
+                send_cols(q, live)
             if j == chunks[k][-1]:
                 store_pack(q, k, packed)
                 packed = zero
-                send_chunk(q, k)
+                send_chunk(q, k, live)
         wait_sends(p)
 
     for k, chunk in enumerate(chunks):
@@ -243,9 +244,6 @@
         return carry
 
     lax.fori_loop(0, steps // 2, two_steps, 0)
-    for k in range(len(chunks)):
-        wait_recv(0, k)
-    wait_sends(0)
     wait_outs(0)
     stores = [pltpu.make_async_copy(cs.at[side, j], c_last.at[column(side, j)], init_sem.at[1, side, j]) for side in range(2) for j in range(tiles)]
     for copy in stores:
@@ -289,7 +287,7 @@
                 dma((2, 2)), dma((2, 2)), dma((2, 8)), dma((2, 8)),
                 dma((2, len(chunks) - 1, 2)), dma((2, len(chunks) - 1, 2)),
             ],
-            compiler_params=pltpu.CompilerParams(collective_id=0, has_side_effects=True, vmem_limit_bytes=60 * 1024 * 1024),
+            compiler_params=pltpu.CompilerParams(collective_id=0, has_side_effects=True, vmem_limit_bytes=12 * 1024 * 1024),
         )(h_in, c_in, w, gate_bias)
         return jnp.transpose(h_seq, (0, 3, 1, 2))[:, None], jnp.transpose(c_last, (2, 0, 1))[None]
 

time: 167 us -> 355 us (2.13)
  Pallas kernels: 148 us -> 343 us
  local copies, waits for them, and re-layouts: 16.9 us -> 11.3 us
    pallas_call x1, Pallas kernels: 148 us -> 343 us  [device_fn(): pl.pallas_call(functools.partial(kernel, steps, tiles, chunks, rows_n, co...]
    unnamed x5 -> x9, local copies, waits for them, and re-layouts: 16 us -> 11.1 us
where the time goes in v3:
time: 355 us
  Pallas kernels  343 us (97%)
  local copies, waits for them, and re-layouts  11.3 us (3%)
    pallas_call x1, Pallas kernels, device_fn(): pl.pallas_call(functools.partial(kernel, steps, tiles, chunks, rows_n, co...  343 us
    unnamed x9, local copies, waits for them, and re-layouts  11.1 us

profile of v3, /device:TPU:0, one launch (start us, length us, event | category | flops | bytes accessed | tf_op | source)
XLA Modules:
  0.0 354.7 jit_solution(6040692976493371571)
XLA Ops:
  0.6 1.0 copy.8
  1.6 0.2 copy.9.w_ref
  1.8 0.0 copy-start
  1.8 1.2 copy-done
  3.0 0.0 copy-start.1
  3.0 1.0 copy-done.1
  4.1 0.0 copy-start.2
  4.1 0.8 copy-done.2
  4.8 342.7 %shard_map.59 = (bf16[32,32,64,128]{3,2,1,0:T(8,128)(2,1)S(1)}, f32[32,64,128]{2,1,0:T(8,128)S(1)}) custom-call(bf16[32,64,128]{2,1,0:T(8,128)(2,1)S(1)} %bitcast.20, f32[32,64,128]{2,1,0:T(8,128)S(1)} %bitcast.19, bf16[256,576]{1,0:T(8,128)(2,1)S(1)} %copy.9.w_ref, f32[32,256]{1,0:T(8,128)S(1)} %copy-done.2), custom_call_target="tpu_custom_call" | custom-call | tf_op jit(solution)/shard_map/pallas_call | solution.py:270
  347.5 6.2 %copy.13 = bf16[32,1,128,32,64]{2,4,3,1,0:T(8,128)(2,1)} copy(bf16[32,1,128,32,64]{2,4,3,1,0:T(8,128)(2,1)S(1)} %bitcast.17) | data formatting | bytes 33554432
  353.7 1.0 copy.14
Async XLA Ops:
  1.8 1.2 copy-start
  3.0 1.0 copy-start.1
  4.1 0.8 copy-start.2

commit v4 on v3

--- a/solution.py
+++ b/solution.py
@@ -15,8 +15,8 @@
 
 
 def kernel(steps, tiles, chunks, rows_n, cols_n, h_init, c_init, w_ref, bias_ref, h_seq, c_last,
-           hl0, hr0, hl1, hr1, cs, ws, bs, ghost, pack_e, pack_c, recv_e, recv_c,
-           init_sem, out_sem, send_col, recv_col, send_e, recv_e_sem, send_c, recv_c_sem):
+           hl0, hr0, hl1, hr1, ws, bs, ghost, pack_e, pack_c, recv_e, recv_c,
+           send_col, recv_col, send_e, recv_e_sem, send_c, recv_c_sem):
     ch, lanes = h_init.shape[1], h_init.shape[2]
     cols = 2 * tiles
     groups = ch // 16
@@ -46,15 +46,10 @@
     def column(side, j):
         return j if side == 0 else cols - 1 - j
 
-    loads = []
     for side in range(2):
         for j in range(tiles):
-            loads.append(pltpu.make_async_copy(h_init.at[column(side, j)], stacks[0][side].at[j + 1, pl.ds(ch, ch)], init_sem.at[0, side, j]))
-            loads.append(pltpu.make_async_copy(c_init.at[column(side, j)], cs.at[side, j], init_sem.at[1, side, j]))
-    for copy in loads:
-        copy.start()
-    for copy in loads:
-        copy.wait()
+            stacks[0][side][j + 1, pl.ds(ch, ch)] = h_init[column(side, j)]
+    c_last[...] = c_init[...]
 
     ws[pl.ds(0, 3 * ch), :] = w_ref[pl.ds(0, 3 * ch), :] * jnp.bfloat16(0.5)
     ws[pl.ds(3 * ch, ch), :] = w_ref[pl.ds(3 * ch, ch), :]
@@ -173,17 +168,9 @@
     def update(side, j, gates):
         part = gates[:, side * lanes:(side + 1) * lanes] + bs[...]
         in_t, forget_t, out_t, cand = (part[ch * b:ch * b + ch] for b in range(4))
-        c = (0.5 * jnp.tanh(forget_t) + 0.5) * cs[side, j] + (0.5 * jnp.tanh(in_t) + 0.5) * jnp.tanh(cand)
-        cs[side, j] = c
+        c = (0.5 * jnp.tanh(forget_t) + 0.5) * c_last[column(side, j)] + (0.5 * jnp.tanh(in_t) + 0.5) * jnp.tanh(cand)
+        c_last[column(side, j)] = c
         return ((0.5 * jnp.tanh(out_t) + 0.5) * jnp.tanh(c)).astype(jnp.bfloat16)
-
-    def out_copy(p, t, side, j):
-        return pltpu.make_async_copy(stacks[p][side].at[j + 1, pl.ds(ch, ch)], h_seq.at[t, column(side, j)], out_sem.at[p, side, j])
-
-    def wait_outs(p):
-        for side in range(2):
-            for j in range(tiles):
-                out_copy(p, 0, side, j).wait()
 
     def store_pack(p, k, packed):
         if k == 0:
@@ -211,9 +198,8 @@
             for side in range(2):
                 h = update(side, j, gates)
                 stacks[q][side][j + 1, pl.ds(ch, ch)] = h
+                h_seq[t, column(side, j)] = h
                 packed = pack(packed, local, side, h)
-            for side in range(2):
-                out_copy(q, t, side, j).start()
             if j == 0:
                 send_cols(q, live)
             if j == chunks[k][-1]:
@@ -234,22 +220,10 @@
 
     def two_steps(i, carry):
         step(2 * i, 0)
-
-        @pl.when(i > 0)
-        def _():
-            wait_outs(0)
-
         step(2 * i + 1, 1)
-        wait_outs(1)
         return carry
 
     lax.fori_loop(0, steps // 2, two_steps, 0)
-    wait_outs(0)
-    stores = [pltpu.make_async_copy(cs.at[side, j], c_last.at[column(side, j)], init_sem.at[1, side, j]) for side in range(2) for j in range(tiles)]
-    for copy in stores:
-        copy.start()
-    for copy in stores:
-        copy.wait()
 
 
 def solution(mesh):
@@ -264,18 +238,16 @@
         h_in = jnp.transpose(h_init[0], (1, 2, 0))
         c_in = jnp.transpose(c_init[0], (1, 2, 0))
         stack = pltpu.VMEM((tiles + 1, 3 * ch, height), jnp.bfloat16)
-        any_spec = pl.BlockSpec(memory_space=pl.ANY)
         vmem_spec = pl.BlockSpec(memory_space=pltpu.VMEM)
         dma = pltpu.SemaphoreType.DMA
         h_seq, c_last = pl.pallas_call(
             functools.partial(kernel, steps, tiles, chunks, rows_n, cols_n),
             out_shape=(jax.ShapeDtypeStruct((steps, width, ch, height), jnp.bfloat16),
                        jax.ShapeDtypeStruct((width, ch, height), jnp.float32)),
-            in_specs=[any_spec, any_spec, vmem_spec, vmem_spec],
-            out_specs=(any_spec, any_spec),
+            in_specs=[vmem_spec] * 4,
+            out_specs=(vmem_spec, vmem_spec),
             scratch_shapes=[
                 stack, stack, stack, stack,
-                pltpu.VMEM((2, tiles, ch, height), jnp.float32),
                 pltpu.VMEM((gates_n, 9 * ch), jnp.bfloat16),
                 pltpu.VMEM((gates_n, height), jnp.float32),
                 pltpu.VMEM((2, 2, ch, height), jnp.bfloat16),
@@ -283,11 +255,10 @@
                 pltpu.VMEM((2, len(chunks) - 1, 16, height), jnp.bfloat16),
                 pltpu.VMEM((2, 8, 16, height), jnp.bfloat16),
                 pltpu.VMEM((2, len(chunks) - 1, 2, 16, height), jnp.bfloat16),
-                dma((2, 2, tiles)), dma((2, 2, tiles)),
                 dma((2, 2)), dma((2, 2)), dma((2, 8)), dma((2, 8)),
                 dma((2, len(chunks) - 1, 2)), dma((2, len(chunks) - 1, 2)),
             ],
-            compiler_params=pltpu.CompilerParams(collective_id=0, has_side_effects=True, vmem_limit_bytes=12 * 1024 * 1024),
+            compiler_params=pltpu.CompilerParams(collective_id=0, has_side_effects=True, vmem_limit_bytes=32 * 1024 * 1024),
         )(h_in, c_in, w, gate_bias)
         return jnp.transpose(h_seq, (0, 3, 1, 2))[:, None], jnp.transpose(c_last, (2, 0, 1))[None]
 

time: 355 us -> 155 us (0.44)
  Pallas kernels: 343 us -> 142 us
    pallas_call x1, Pallas kernels: 343 us -> 142 us  [device_fn(): pl.pallas_call(functools.partial(kernel, steps, tiles, chunks, rows_n, co...]
where the time goes in v4:
time: 155 us; the launch traced here: 154 us
  Pallas kernels  142 us (92%)
  local copies, waits for them, and re-layouts  11.3 us (7%)
    pallas_call x1, Pallas kernels, device_fn(): pl.pallas_call(functools.partial(kernel, steps, tiles, chunks, rows_n, co...  142 us
    unnamed x9, local copies, waits for them, and re-layouts  11.1 us

profile of v4, /device:TPU:0, one launch (start us, length us, event | category | flops | bytes accessed | tf_op | source)
XLA Modules:
  0.0 153.9 jit_solution(16188399100824354737)
XLA Ops:
  0.6 1.0 copy.8
  1.6 0.2 copy.9.w_ref
  1.8 0.0 copy-start
  1.8 1.2 copy-done
  3.0 0.0 copy-start.1
  3.0 1.0 copy-done.1
  4.1 0.0 copy-start.2
  4.1 0.8 copy-done.2
  4.8 141.9 %shard_map.59 = (bf16[32,32,64,128]{3,2,1,0:T(8,128)(2,1)S(1)}, f32[32,64,128]{2,1,0:T(8,128)S(1)}) custom-call(bf16[32,64,128]{2,1,0:T(8,128)(2,1)S(1)} %bitcast.20, f32[32,64,128]{2,1,0:T(8,128)S(1)} %bitcast.19, bf16[256,576]{1,0:T(8,128)(2,1)S(1)} %copy.9.w_ref, f32[32,256]{1,0:T(8,128)S(1)} %copy-done.2), custom_call_target="tpu_custom_call" | custom-call | tf_op jit(solution)/shard_map/pallas_call | solution.py:243
  146.8 6.2 %copy.13 = bf16[32,1,128,32,64]{2,4,3,1,0:T(8,128)(2,1)} copy(bf16[32,1,128,32,64]{2,4,3,1,0:T(8,128)(2,1)S(1)} %bitcast.17) | data formatting | bytes 33554432
  152.9 1.0 copy.14
Async XLA Ops:
  1.8 1.2 copy-start
  3.0 1.0 copy-start.1
  4.1 0.8 copy-start.2

commit v5 on v0

v5 whole, which is shorter than its diff:
```python
import functools

import jax
import jax.numpy as jnp
from jax import lax
from jax.experimental import pallas as pl
from jax.experimental.pallas import tpu as pltpu
from jax.sharding import PartitionSpec as P

UP, DOWN, LEFT, RIGHT, UP_LEFT, UP_RIGHT, DOWN_LEFT, DOWN_RIGHT = range(8)
OFFSETS = ((-1, 0), (1, 0), (0, -1), (0, 1), (-1, -1), (-1, 1), (1, -1), (1, 1))
OPPOSITE = (DOWN, UP, RIGHT, LEFT, DOWN_RIGHT, DOWN_LEFT, UP_RIGHT, UP_LEFT)
DIAGONALS = (UP_LEFT, UP_RIGHT, DOWN_LEFT, DOWN_RIGHT)
MESH = pl.DeviceIdType.MESH


def kernel(steps, tiles, rows_n, cols_n, h_init, c_init, w_ref, bias_ref, h_seq, c_last,
           hl0, hr0, hl1, hr1, ws, bs, c_strip, inner, strip, corner, ghost, recv_s, recv_d,
           send_col, recv_col, send_strip, recv_strip, send_diag, recv_diag):
    ch, lanes = h_init.shape[1], h_init.shape[2]
    cols = 2 * tiles
    groups = range(ch // 16)
    stacks = ((hl0, hr0), (hl1, hr1))
    row, col = lax.axis_index("rows"), lax.axis_index("cols")

    has, target = [], []
    for dr, dc in OFFSETS:
        r, c = row + dr, col + dc
        has.append((r >= 0) & (r < rows_n) & (c >= 0) & (c < cols_n))
        target.append({"rows": r, "cols": c})

    def at(d, action, live=None):
        pl.when(has[d] if live is None else has[d] & live)(action)

    for ref in (ghost, recv_s, recv_d):
        ref[...] = jnp.zeros_like(ref)
    barrier = pltpu.get_barrier_semaphore()
    for d in range(8):
        at(d, lambda d=d: pl.semaphore_signal(barrier, inc=1, device_id=target[d], device_id_type=MESH))
    around_r = 1 + has[UP].astype(jnp.int32) + has[DOWN].astype(jnp.int32)
    around_c = 1 + has[LEFT].astype(jnp.int32) + has[RIGHT].astype(jnp.int32)
    pl.semaphore_wait(barrier, around_r * around_c - 1)

    def column(side, j):
        return j if side == 0 else cols - 1 - j

    ws[pl.ds(0, 3 * ch), :] = w_ref[pl.ds(0, 3 * ch), :] * jnp.bfloat16(0.5)
    ws[pl.ds(3 * ch, ch), :] = w_ref[pl.ds(3 * ch, ch), :]
    scale = jnp.where(lax.broadcasted_iota(jnp.int32, (1, 4 * ch), 1) < 3 * ch, 0.5, 1.0).astype(jnp.float32)
    c_last[...] = c_init[...]

    lane = lax.broadcasted_iota(jnp.int16, (16, lanes), 1)
    lane32 = lax.broadcasted_iota(jnp.int32, (8, lanes), 1)
    even = (lane & jnp.int16(1)) == jnp.int16(0)
    ends = (lane == jnp.int16(0)) | (lane == jnp.int16(lanes - 1))

    def is_lane(n):
        return lane == jnp.int16(n)

    def roll(x, n):
        return pltpu.roll(x, n % lanes, 1) if n % lanes else x

    def part(x, g):
        return x[16 * g:16 * g + 16]

    def col_copy(p, d):
        return pltpu.make_async_remote_copy(
            src_ref=stacks[p][d - LEFT].at[1, pl.ds(ch, ch)], dst_ref=ghost.at[p, OPPOSITE[d] - LEFT],
            send_sem=send_col.at[p, d - LEFT], recv_sem=recv_col.at[p, OPPOSITE[d] - LEFT], device_id=target[d], device_id_type=MESH)

    def strip_copy(p, d):
        return pltpu.make_async_remote_copy(
            src_ref=strip.at[p], dst_ref=recv_s.at[p, OPPOSITE[d]],
            send_sem=send_strip.at[p, d], recv_sem=recv_strip.at[p, OPPOSITE[d]], device_id=target[d], device_id_type=MESH)

    def diag_copy(p, d):
        return pltpu.make_async_remote_copy(
            src_ref=corner.at[p], dst_ref=recv_d.at[p, OPPOSITE[d] - UP_LEFT],
            send_sem=send_diag.at[p, d - UP_LEFT], recv_sem=recv_diag.at[p, OPPOSITE[d] - UP_LEFT], device_id=target[d], device_id_type=MESH)

    def wait_block(ref, sem):
        pltpu.make_async_copy(ref, ref, sem).wait()

    def send_cols(p, live=None):
        for d in (LEFT, RIGHT):
            at(d, lambda d=d: col_copy(p, d).start(), live)

    def send_strip_to(p, live=None):
        for d in DIAGONALS:
            at(d, lambda d=d: diag_copy(p, d).start(), live)
        for d in (UP, DOWN):
            at(d, lambda d=d: strip_copy(p, d).start(), live)

    def wait_sends(p):
        for d in (LEFT, RIGHT):
            at(d, lambda d=d: col_copy(p, d).wait_send())
        for d in DIAGONALS:
            at(d, lambda d=d: diag_copy(p, d).wait_send())
        for d in (UP, DOWN):
            at(d, lambda d=d: strip_copy(p, d).wait_send())

    def wait_recv(p):
        for d in (UP, DOWN):
            at(d, lambda d=d: wait_block(recv_s.at[p, d], recv_strip.at[p, d]))
        for d in DIAGONALS:
            at(d, lambda d=d: wait_block(recv_d.at[p, d - UP_LEFT], recv_diag.at[p, d - UP_LEFT]))
        for d in (LEFT, RIGHT):
            at(d, lambda d=d: wait_block(ghost.at[p, d - LEFT], recv_col.at[p, d - LEFT]))

    def store_column(dst, s, g, h):
        dst[s, pl.ds(16 * g, 16)] = roll(h, 1)
        dst[s, pl.ds(ch + 16 * g, 16)] = h
        dst[s, pl.ds(2 * ch + 16 * g, 16)] = roll(h, -1)

    def add_inner(packed, x, h):
        return jnp.where(is_lane(2 * x + 3) | is_lane(2 * x + 6), roll(h, 2 * x + 5), packed)

    def store_strip(p, h):
        strip[p] = h
        block = part(h, 0)
        for g in groups[1:]:
            block = jnp.where(lax.shift_right_logical(lane & jnp.int16(63), jnp.int16(3)) == jnp.int16(g), roll(part(h, g), 8 * g), block)
        corner[p] = block

    def gates_of(stack):
        return jnp.dot(ws[...], stack, preferred_element_type=jnp.float32)

    def update(gates, c_prev):
        pre = gates + bs[...]
        in_t, forget_t, out_t, cand = (pre[ch * b:ch * b + ch] for b in range(4))
        c = (0.5 * jnp.tanh(forget_t) + 0.5) * c_prev + (0.5 * jnp.tanh(in_t) + 0.5) * jnp.tanh(cand)
        return ((0.5 * jnp.tanh(out_t) + 0.5) * jnp.tanh(c)).astype(jnp.bfloat16), c

    def strip_stack(p):
        above, here, below = [], [], []
        for g in groups:
            rows = pl.ds(16 * g, 16)
            packed, own = inner[rows], strip[p, rows]
            for side, x in ((0, -1), (1, cols)):
                h = ghost[p, side, rows]
                store_column(stacks[p][side], 0, g, h)
                packed = add_inner(packed, x, h)
                own = jnp.where(is_lane(2 * x + 6), roll(h, 2 * x + 6), own)
                own = jnp.where(is_lane(2 * x + 3), roll(h, 2 * x + 4), own)
            up = jnp.where(even, roll(recv_s[p, UP, rows], 3), packed)
            down = jnp.where(even, packed, roll(recv_s[p, DOWN, rows], -3))
            diag = [recv_d[p, k] for k in range(4)]
            up = jnp.where(is_lane(4), roll(diag[0], 4 - 65 - 8 * g), up)
            up = jnp.where(is_lane(2 * cols + 6), roll(diag[1], 2 * cols + 6 - 3 - 8 * g), up)
            down = jnp.where(is_lane(1), roll(diag[2], 1 - 68 - 8 * g), down)
            down = jnp.where(is_lane(2 * cols + 3), roll(diag[3], 2 * cols + 3 - 6 - 8 * g), down)
            above.append(up)
            here.append(own)
            below.append(down)
        rows = above + here + below
        return jnp.concatenate([roll(v, 2) for v in rows] + rows + [roll(v, -2) for v in rows], axis=0)

    def matmul(p, j):
        left, right = stacks[p]
        l_next = left[j + 2] if j + 1 < tiles else right[tiles]
        r_next = right[j + 2] if j + 1 < tiles else left[tiles]
        stack_l = jnp.concatenate([left[j], left[j + 1], l_next], axis=0)
        stack_r = jnp.concatenate([r_next, right[j + 1], right[j]], axis=0)
        return gates_of(jnp.concatenate([stack_l, stack_r], axis=1))

    def step(t, p):
        q = 1 - p
        live = t < steps - 1 if p else None
        line = bias_ref[pl.ds(t, 1), :] * scale
        bs[...] = jnp.transpose(jnp.broadcast_to(line, (lanes, line.shape[1])))
        wait_recv(p)
        hs, cs = update(gates_of(strip_stack(p)), c_strip[...])
        c_strip[...] = cs
        store_strip(q, hs)
        send_strip_to(q, live)
        merged = [jnp.where(even, part(hs, g), roll(part(hs, g), 2)) for g in groups]
        packed = [jnp.zeros((16, lanes), jnp.bfloat16) for _ in groups]
        for j in range(tiles):
            gates = matmul(p, j)
            for side in range(2):
                x = column(side, j)
                h, c = update(gates[:, side * lanes:(side + 1) * lanes], c_last[x])
                c_last[x] = c
                for g in groups:
                    fixed = jnp.where(ends, roll(merged[g], -(2 * x + 6)), part(h, g))
                    store_column(stacks[q][side], j + 1, g, fixed)
                    h_seq[t, x, pl.ds(16 * g, 16)] = fixed
                    packed[g] = add_inner(packed[g], x, fixed)
            if j == 0:
                send_cols(q, live)
        for g in groups:
            inner[pl.ds(16 * g, 16)] = packed[g]
        wait_sends(p)

    packed = [jnp.zeros((16, lanes), jnp.bfloat16) for _ in groups]
    edge = [jnp.zeros((16, lanes), jnp.bfloat16) for _ in groups]
    c_edge = [jnp.zeros((8, lanes), jnp.float32) for _ in range(ch // 8)]
    for j in range(tiles):
        for side in range(2):
            x = column(side, j)
            for g in groups:
                h = h_init[x, pl.ds(16 * g, 16)]
                store_column(stacks[0][side], j + 1, g, h)
                packed[g] = add_inner(packed[g], x, h)
                edge[g] = jnp.where(is_lane(2 * x + 5) | is_lane(2 * x + 6), roll(h, 2 * x + 6), edge[g])
            for g in range(ch // 8):
                c = roll(c_init[x, pl.ds(8 * g, 8)], 2 * x + 6)
                c_edge[g] = jnp.where((lane32 == 2 * x + 5) | (lane32 == 2 * x + 6), c, c_edge[g])
    for g in groups:
        inner[pl.ds(16 * g, 16)] = packed[g]
    for g in range(ch // 8):
        c_strip[pl.ds(8 * g, 8)] = jnp.where((lane32 & 1) == 0, c_edge[g], roll(c_edge[g], -2))
    store_strip(0, jnp.concatenate([jnp.where(even, e, roll(e, -2)) for e in edge], axis=0))
    send_strip_to(0)
    send_cols(0)

    def two_steps(i, carry):
        step(2 * i, 0)
        step(2 * i + 1, 1)
        return carry

    lax.fori_loop(0, steps // 2, two_steps, 0)
    for g in range(ch // 8):
        c = c_strip[pl.ds(8 * g, 8)]
        c = jnp.where((lane32 & 1) == 0, c, roll(c, 2))
        for x in range(cols):
            rows = pl.ds(8 * g, 8)
            c_last[x, rows] = jnp.where((lane32 == 0) | (lane32 == lanes - 1), roll(c, -(2 * x + 6)), c_last[x, rows])


def solution(mesh):
    rows_n, cols_n = mesh.shape["rows"], mesh.shape["cols"]

    def device_fn(h_init, c_init, w_rec, gate_bias):
        _, height, width, ch = h_init.shape
        steps, gates_n = gate_bias.shape
        tiles = width // 2
        w = jnp.transpose(w_rec, (3, 1, 0, 2)).reshape(gates_n, 9 * ch)
        h_in = jnp.transpose(h_init[0], (1, 2, 0))
        c_in = jnp.transpose(c_init[0], (1, 2, 0))
        stack = pltpu.VMEM((tiles + 1, 3 * ch, height), jnp.bfloat16)
        vmem_spec = pl.BlockSpec(memory_space=pltpu.VMEM)
        dma = pltpu.SemaphoreType.DMA
        h_seq, c_last = pl.pallas_call(
            functools.partial(kernel, steps, tiles, rows_n, cols_n),
            out_shape=(jax.ShapeDtypeStruct((steps, width, ch, height), jnp.bfloat16),
                       jax.ShapeDtypeStruct((width, ch, height), jnp.float32)),
            in_specs=[vmem_spec] * 4,
            out_specs=(vmem_spec, vmem_spec),
            scratch_shapes=[
                stack, stack, stack, stack,
                pltpu.VMEM((gates_n, 9 * ch), jnp.bfloat16),
                pltpu.VMEM((gates_n, height), jnp.float32),
                pltpu.VMEM((ch, height), jnp.float32),
                pltpu.VMEM((ch, height), jnp.bfloat16),
                pltpu.VMEM((2, ch, height), jnp.bfloat16),
                pltpu.VMEM((2, 16, height), jnp.bfloat16),
                pltpu.VMEM((2, 2, ch, height), jnp.bfloat16),
                pltpu.VMEM((2, 2, ch, height), jnp.bfloat16),
                pltpu.VMEM((2, 4, 16, height), jnp.bfloat16),
                dma((2, 2)), dma((2, 2)), dma((2, 2)), dma((2, 2)), dma((2, 4)), dma((2, 4)),
            ],
            compiler_params=pltpu.CompilerParams(collective_id=0, has_side_effects=True, vmem_limit_bytes=32 * 1024 * 1024),
        )(h_in, c_in, w, gate_bias)
        return jnp.transpose(h_seq, (0, 3, 1, 2))[:, None], jnp.transpose(c_last, (2, 0, 1))[None]

    state_spec = P("dp", "rows", "cols", None)
    return jax.shard_map(device_fn, mesh=mesh, in_specs=(state_spec, state_spec, P(), P()), out_specs=(P(None, "dp", "rows", "cols", None), state_spec), check_vma=False)
```

time: 1330 us -> 139 us (0.10); the launches traced: 1310 us -> 139 us
  starting transfers between devices: 538 us -> 0 us
  local copies, waits for them, and re-layouts: 334 us -> 11.3 us
  other arithmetic: 210 us -> 0 us
  matrix products: 146 us -> 0 us
  Pallas kernels: 0 us -> 127 us
  waiting for transfers between devices: 75.1 us -> 0 us
    ppermute x128 -> x0, starting transfers between devices: 538 us -> none  [the longest x32 309 us: with_halo(): from_above = lax.ppermute(tile[:, -1:], 'rows', rows_down)]
    conv_general_dilated x96 -> x0, local copies, waits for them, and re-layouts: 262 us -> none  [one_step(): lax.conv_general_dilated(padded, w_rec, (1, 1), 'VALID', dimension_number...]
    conv_general_dilated x32 -> x0, matrix products: 146 us -> none  [one_step(): lax.conv_general_dilated(padded, w_rec, (1, 1), 'VALID', dimension_number...]
    pallas_call x0 -> x1, Pallas kernels: none -> 127 us  [device_fn(): pl.pallas_call(functools.partial(kernel, steps, tiles, rows_n, cols_n), o...]
    add x32 -> x0, other arithmetic: 103 us -> none  [one_step(): lax.conv_general_dilated(padded, w_rec, (1, 1), 'VALID', dimension_number...]
    ppermute x128 -> x0, waiting for transfers between devices: 75.1 us -> none  [the longest x32 47.2 us: with_halo(): from_above = lax.ppermute(tile[:, -1:], 'rows', rows_down)]
    dynamic_update_slice x32 -> x0, other arithmetic: 44.9 us -> none  [device_fn(): final_state, h_seq = lax.scan(one_step, (h_init, c_init), gate_bias)]
    div x32 -> x0, other arithmetic: 38.2 us -> none  [lstm_update(): jax.nn.sigmoid(forget_gate) * c_prev]
  transfers between devices with their start and end apart: 128 -> 0, of which waited for: 64 -> 0; matrix products, arithmetic and copies ran while one was open for 2% -> 0% of each run, Pallas kernels for 0% -> 0%
where the time goes in v5:
time: 139 us
  Pallas kernels  127 us (91%)
  local copies, waits for them, and re-layouts  11.3 us (8%)
    pallas_call x1, Pallas kernels, device_fn(): pl.pallas_call(functools.partial(kernel, steps, tiles, rows_n, cols_n), o...  127 us
    unnamed x9, local copies, waits for them, and re-layouts  11.1 us

profile of v5, /device:TPU:0, one launch (start us, length us, event | category | flops | bytes accessed | tf_op | source)
XLA Modules:
  0.0 138.8 jit_solution(300113632459802007)
XLA Ops:
  0.6 1.0 copy.8
  1.6 0.2 copy.9.w_ref
  1.8 0.0 copy-start
  1.8 1.2 copy-done
  3.0 0.0 copy-start.1
  3.0 1.0 copy-done.1
  4.1 0.0 copy-start.2
  4.1 0.8 copy-done.2
  4.8 126.8 %shard_map.59 = (bf16[32,32,64,128]{3,2,1,0:T(8,128)(2,1)S(1)}, f32[32,64,128]{2,1,0:T(8,128)S(1)}) custom-call(bf16[32,64,128]{2,1,0:T(8,128)(2,1)S(1)} %bitcast.20, f32[32,64,128]{2,1,0:T(8,128)S(1)} %bitcast.19, bf16[256,576]{1,0:T(8,128)(2,1)S(1)} %copy.9.w_ref, f32[32,256]{1,0:T(8,128)S(1)} %copy-done.2), custom_call_target="tpu_custom_call" | custom-call | tf_op jit(solution)/shard_map/pallas_call | solution.py:244
  131.7 6.2 %copy.13 = bf16[32,1,128,32,64]{2,4,3,1,0:T(8,128)(2,1)} copy(bf16[32,1,128,32,64]{2,4,3,1,0:T(8,128)(2,1)S(1)} %bitcast.17) | data formatting | bytes 33554432
  137.9 1.0 copy.14
Async XLA Ops:
  1.8 1.2 copy-start
  3.0 1.0 copy-start.1
  4.1 0.8 copy-start.2

commit v6 on v5

--- a/solution.py
+++ b/solution.py
@@ -14,9 +14,9 @@
 MESH = pl.DeviceIdType.MESH
 
 
-def kernel(steps, tiles, rows_n, cols_n, h_init, c_init, w_ref, bias_ref, h_seq, c_last,
-           hl0, hr0, hl1, hr1, ws, bs, c_strip, inner, strip, corner, ghost, recv_s, recv_d,
-           send_col, recv_col, send_strip, recv_strip, send_diag, recv_diag):
+def kernel(steps, tiles, rows_n, cols_n, h_init, c_init, w_ref, bias_in, h_seq, c_last,
+           hl0, hr0, hl1, hr1, ws, bias_ref, bs, c_strip, inner, strip, corner, ghost, recv_s, recv_d,
+           init_sem, send_col, recv_col, send_strip, recv_strip, send_diag, recv_diag):
     ch, lanes = h_init.shape[1], h_init.shape[2]
     cols = 2 * tiles
     groups = range(ch // 16)
@@ -31,6 +31,14 @@
 
     def at(d, action, live=None):
         pl.when(has[d] if live is None else has[d] & live)(action)
+
+    loads = [pltpu.make_async_copy(c_init, c_last, init_sem.at[0]), pltpu.make_async_copy(bias_in, bias_ref, init_sem.at[1])]
+    for side in range(2):
+        for j in range(tiles):
+            x = j if side == 0 else cols - 1 - j
+            loads.append(pltpu.make_async_copy(h_init.at[x], stacks[0][side].at[j + 1, pl.ds(ch, ch)], init_sem.at[2 + x]))
+    for copy in loads:
+        copy.start()
 
     for ref in (ghost, recv_s, recv_d):
         ref[...] = jnp.zeros_like(ref)
@@ -47,7 +55,8 @@
     ws[pl.ds(0, 3 * ch), :] = w_ref[pl.ds(0, 3 * ch), :] * jnp.bfloat16(0.5)
     ws[pl.ds(3 * ch, ch), :] = w_ref[pl.ds(3 * ch, ch), :]
     scale = jnp.where(lax.broadcasted_iota(jnp.int32, (1, 4 * ch), 1) < 3 * ch, 0.5, 1.0).astype(jnp.float32)
-    c_last[...] = c_init[...]
+    for copy in loads:
+        copy.wait()
 
     lane = lax.broadcasted_iota(jnp.int16, (16, lanes), 1)
     lane32 = lax.broadcasted_iota(jnp.int32, (8, lanes), 1)
@@ -131,29 +140,32 @@
         c = (0.5 * jnp.tanh(forget_t) + 0.5) * c_prev + (0.5 * jnp.tanh(in_t) + 0.5) * jnp.tanh(cand)
         return ((0.5 * jnp.tanh(out_t) + 0.5) * jnp.tanh(c)).astype(jnp.bfloat16), c
 
-    def strip_stack(p):
-        above, here, below = [], [], []
+    def strip_parts(p):
+        own = [[roll(strip[p, pl.ds(16 * g, 16)], n) for n in (2, 0, -2)] for g in groups]
+        near = [[roll(inner[pl.ds(16 * g, 16)], n) for n in (2, 0, -2)] for g in groups]
+        return own, near
+
+    def strip_stack(p, own, near):
+        blocks = [[[], [], []] for _ in range(3)]
         for g in groups:
             rows = pl.ds(16 * g, 16)
-            packed, own = inner[rows], strip[p, rows]
-            for side, x in ((0, -1), (1, cols)):
-                h = ghost[p, side, rows]
-                store_column(stacks[p][side], 0, g, h)
-                packed = add_inner(packed, x, h)
-                own = jnp.where(is_lane(2 * x + 6), roll(h, 2 * x + 6), own)
-                own = jnp.where(is_lane(2 * x + 3), roll(h, 2 * x + 4), own)
-            up = jnp.where(even, roll(recv_s[p, UP, rows], 3), packed)
-            down = jnp.where(even, packed, roll(recv_s[p, DOWN, rows], -3))
-            diag = [recv_d[p, k] for k in range(4)]
-            up = jnp.where(is_lane(4), roll(diag[0], 4 - 65 - 8 * g), up)
-            up = jnp.where(is_lane(2 * cols + 6), roll(diag[1], 2 * cols + 6 - 3 - 8 * g), up)
-            down = jnp.where(is_lane(1), roll(diag[2], 1 - 68 - 8 * g), down)
-            down = jnp.where(is_lane(2 * cols + 3), roll(diag[3], 2 * cols + 3 - 6 - 8 * g), down)
-            above.append(up)
-            here.append(own)
-            below.append(down)
-        rows = above + here + below
-        return jnp.concatenate([roll(v, 2) for v in rows] + rows + [roll(v, -2) for v in rows], axis=0)
+            for k, n in enumerate((2, 0, -2)):
+                here, packed = own[g][k], near[g][k]
+                up, down = roll(recv_s[p, UP, rows], 3 + n), roll(recv_s[p, DOWN, rows], n - 3)
+                if n:
+                    side, x = (0, -1) if n > 0 else (1, cols)
+                    top, bottom = 2 * x + 6 + n, 2 * x + 3 + n
+                    h = ghost[p, side, rows]
+                    here = jnp.where(is_lane(top), roll(h, top), here)
+                    here = jnp.where(is_lane(bottom), roll(h, bottom + 1), here)
+                    packed = jnp.where(is_lane(top) | is_lane(bottom), roll(h, top - 1), packed)
+                    far = 62 if side == 0 else 0
+                    up = jnp.where(is_lane(top), roll(recv_d[p, side], top - 3 - far - 8 * g), up)
+                    down = jnp.where(is_lane(bottom), roll(recv_d[p, 2 + side], bottom - 6 - far - 8 * g), down)
+                blocks[k][0].append(jnp.where(even, up, packed))
+                blocks[k][1].append(here)
+                blocks[k][2].append(jnp.where(even, packed, down))
+        return jnp.concatenate([v for shift in blocks for block in shift for v in block], axis=0)
 
     def matmul(p, j):
         left, right = stacks[p]
@@ -168,15 +180,21 @@
         live = t < steps - 1 if p else None
         line = bias_ref[pl.ds(t, 1), :] * scale
         bs[...] = jnp.transpose(jnp.broadcast_to(line, (lanes, line.shape[1])))
+        own, near = strip_parts(p)
         wait_recv(p)
-        hs, cs = update(gates_of(strip_stack(p)), c_strip[...])
+        for side in range(2):
+            for g in groups:
+                store_column(stacks[p][side], 0, g, ghost[p, side, pl.ds(16 * g, 16)])
+        strip_gates = gates_of(strip_stack(p, own, near))
+        hs, cs = update(strip_gates, c_strip[...])
         c_strip[...] = cs
         store_strip(q, hs)
-        send_strip_to(q, live)
         merged = [jnp.where(even, part(hs, g), roll(part(hs, g), 2)) for g in groups]
         packed = [jnp.zeros((16, lanes), jnp.bfloat16) for _ in groups]
+        send_strip_to(q, live)
+        gates = matmul(p, 0)
         for j in range(tiles):
-            gates = matmul(p, j)
+            following = matmul(p, j + 1) if 0 < j < tiles - 1 else None
             for side in range(2):
                 x = column(side, j)
                 h, c = update(gates[:, side * lanes:(side + 1) * lanes], c_last[x])
@@ -186,8 +204,10 @@
                     store_column(stacks[q][side], j + 1, g, fixed)
                     h_seq[t, x, pl.ds(16 * g, 16)] = fixed
                     packed[g] = add_inner(packed[g], x, fixed)
+            gates = following
             if j == 0:
                 send_cols(q, live)
+                gates = matmul(p, 1)
         for g in groups:
             inner[pl.ds(16 * g, 16)] = packed[g]
         wait_sends(p)
@@ -199,12 +219,12 @@
         for side in range(2):
             x = column(side, j)
             for g in groups:
-                h = h_init[x, pl.ds(16 * g, 16)]
+                h = stacks[0][side][j + 1, pl.ds(ch + 16 * g, 16)]
                 store_column(stacks[0][side], j + 1, g, h)
                 packed[g] = add_inner(packed[g], x, h)
                 edge[g] = jnp.where(is_lane(2 * x + 5) | is_lane(2 * x + 6), roll(h, 2 * x + 6), edge[g])
             for g in range(ch // 8):
-                c = roll(c_init[x, pl.ds(8 * g, 8)], 2 * x + 6)
+                c = roll(c_last[x, pl.ds(8 * g, 8)], 2 * x + 6)
                 c_edge[g] = jnp.where((lane32 == 2 * x + 5) | (lane32 == 2 * x + 6), c, c_edge[g])
     for g in groups:
         inner[pl.ds(16 * g, 16)] = packed[g]
@@ -239,17 +259,19 @@
         h_in = jnp.transpose(h_init[0], (1, 2, 0))
         c_in = jnp.transpose(c_init[0], (1, 2, 0))
         stack = pltpu.VMEM((tiles + 1, 3 * ch, height), jnp.bfloat16)
+        hbm_spec = pl.BlockSpec(memory_space=pltpu.MemorySpace.HBM)
         vmem_spec = pl.BlockSpec(memory_space=pltpu.VMEM)
         dma = pltpu.SemaphoreType.DMA
         h_seq, c_last = pl.pallas_call(
             functools.partial(kernel, steps, tiles, rows_n, cols_n),
             out_shape=(jax.ShapeDtypeStruct((steps, width, ch, height), jnp.bfloat16),
                        jax.ShapeDtypeStruct((width, ch, height), jnp.float32)),
-            in_specs=[vmem_spec] * 4,
+            in_specs=[hbm_spec, hbm_spec, vmem_spec, hbm_spec],
             out_specs=(vmem_spec, vmem_spec),
             scratch_shapes=[
                 stack, stack, stack, stack,
                 pltpu.VMEM((gates_n, 9 * ch), jnp.bfloat16),
+                pltpu.VMEM((steps, gates_n), jnp.float32),
                 pltpu.VMEM((gates_n, height), jnp.float32),
                 pltpu.VMEM((ch, height), jnp.float32),
                 pltpu.VMEM((ch, height), jnp.bfloat16),
@@ -258,7 +280,7 @@
                 pltpu.VMEM((2, 2, ch, height), jnp.bfloat16),
                 pltpu.VMEM((2, 2, ch, height), jnp.bfloat16),
                 pltpu.VMEM((2, 4, 16, height), jnp.bfloat16),
-                dma((2, 2)), dma((2, 2)), dma((2, 2)), dma((2, 2)), dma((2, 4)), dma((2, 4)),
+                dma((2 + width,)), dma((2, 2)), dma((2, 2)), dma((2, 2)), dma((2, 2)), dma((2, 4)), dma((2, 4)),
             ],
             compiler_params=pltpu.CompilerParams(collective_id=0, has_side_effects=True, vmem_limit_bytes=32 * 1024 * 1024),
         )(h_in, c_in, w, gate_bias)

time: 139 us -> 137 us (0.986)
  Pallas kernels: 127 us -> 125 us
    pallas_call x1, Pallas kernels: 127 us -> 125 us  [device_fn(): pl.pallas_call(functools.partial(kernel, steps, tiles, rows_n, cols_n), o...]
where the time goes in v6:
time: 137 us
  Pallas kernels  125 us (91%)
  local copies, waits for them, and re-layouts  11.3 us (8%)
    pallas_call x1, Pallas kernels, device_fn(): pl.pallas_call(functools.partial(kernel, steps, tiles, rows_n, cols_n), o...  125 us
    unnamed x9, local copies, waits for them, and re-layouts  11.1 us

profile of v6, /device:TPU:0, one launch (start us, length us, event | category | flops | bytes accessed | tf_op | source)
XLA Modules:
  0.0 137.1 jit_solution(13782544047643548709)
XLA Ops:
  0.6 1.0 copy.8
  1.6 0.2 copy.9.w_ref
  1.8 0.0 copy-start
  1.8 1.2 copy-done
  3.0 0.0 copy-start.1
  3.0 1.0 copy-done.1
  4.1 0.0 copy-start.2
  4.1 0.8 copy-done.2
  4.8 125.1 %shard_map.59 = (bf16[32,32,64,128]{3,2,1,0:T(8,128)(2,1)S(1)}, f32[32,64,128]{2,1,0:T(8,128)S(1)}) custom-call(bf16[32,64,128]{2,1,0:T(8,128)(2,1)S(1)} %bitcast.20, f32[32,64,128]{2,1,0:T(8,128)S(1)} %bitcast.19, bf16[256,576]{1,0:T(8,128)(2,1)S(1)} %copy.9.w_ref, f32[32,256]{1,0:T(8,128)S(1)} %copy-done.2), custom_call_target="tpu_custom_call" | custom-call | tf_op jit(solution)/shard_map/pallas_call | solution.py:265
  130.0 6.2 %copy.13 = bf16[32,1,128,32,64]{2,4,3,1,0:T(8,128)(2,1)} copy(bf16[32,1,128,32,64]{2,4,3,1,0:T(8,128)(2,1)S(1)} %bitcast.17) | data formatting | bytes 33554432
  136.2 1.0 copy.14
Async XLA Ops:
  1.8 1.2 copy-start
  3.0 1.0 copy-start.1
  4.1 0.8 copy-start.2

commit v7 on v6

--- a/solution.py
+++ b/solution.py
@@ -14,9 +14,9 @@
 MESH = pl.DeviceIdType.MESH
 
 
-def kernel(steps, tiles, rows_n, cols_n, h_init, c_init, w_ref, bias_in, h_seq, c_last,
-           hl0, hr0, hl1, hr1, ws, bias_ref, bs, c_strip, inner, strip, corner, ghost, recv_s, recv_d,
-           init_sem, send_col, recv_col, send_strip, recv_strip, send_diag, recv_diag):
+def kernel(steps, tiles, rows_n, cols_n, h_init, c_init, w_ref, bias_ref, h_seq, c_last,
+           hl0, hr0, hl1, hr1, ws, bs, c_strip, inner, strip, corner, ghost, recv_s, recv_d,
+           send_col, recv_col, send_strip, recv_strip, send_diag, recv_diag):
     ch, lanes = h_init.shape[1], h_init.shape[2]
     cols = 2 * tiles
     groups = range(ch // 16)
@@ -31,14 +31,6 @@
 
     def at(d, action, live=None):
         pl.when(has[d] if live is None else has[d] & live)(action)
-
-    loads = [pltpu.make_async_copy(c_init, c_last, init_sem.at[0]), pltpu.make_async_copy(bias_in, bias_ref, init_sem.at[1])]
-    for side in range(2):
-        for j in range(tiles):
-            x = j if side == 0 else cols - 1 - j
-            loads.append(pltpu.make_async_copy(h_init.at[x], stacks[0][side].at[j + 1, pl.ds(ch, ch)], init_sem.at[2 + x]))
-    for copy in loads:
-        copy.start()
 
     for ref in (ghost, recv_s, recv_d):
         ref[...] = jnp.zeros_like(ref)
@@ -55,8 +47,7 @@
     ws[pl.ds(0, 3 * ch), :] = w_ref[pl.ds(0, 3 * ch), :] * jnp.bfloat16(0.5)
     ws[pl.ds(3 * ch, ch), :] = w_ref[pl.ds(3 * ch, ch), :]
     scale = jnp.where(lax.broadcasted_iota(jnp.int32, (1, 4 * ch), 1) < 3 * ch, 0.5, 1.0).astype(jnp.float32)
-    for copy in loads:
-        copy.wait()
+    c_last[...] = c_init[...]
 
     lane = lax.broadcasted_iota(jnp.int16, (16, lanes), 1)
     lane32 = lax.broadcasted_iota(jnp.int32, (8, lanes), 1)
@@ -219,12 +210,12 @@
         for side in range(2):
             x = column(side, j)
             for g in groups:
-                h = stacks[0][side][j + 1, pl.ds(ch + 16 * g, 16)]
+                h = h_init[x, pl.ds(16 * g, 16)]
                 store_column(stacks[0][side], j + 1, g, h)
                 packed[g] = add_inner(packed[g], x, h)
                 edge[g] = jnp.where(is_lane(2 * x + 5) | is_lane(2 * x + 6), roll(h, 2 * x + 6), edge[g])
             for g in range(ch // 8):
-                c = roll(c_last[x, pl.ds(8 * g, 8)], 2 * x + 6)
+                c = roll(c_init[x, pl.ds(8 * g, 8)], 2 * x + 6)
                 c_edge[g] = jnp.where((lane32 == 2 * x + 5) | (lane32 == 2 * x + 6), c, c_edge[g])
     for g in groups:
         inner[pl.ds(16 * g, 16)] = packed[g]
@@ -259,19 +250,17 @@
         h_in = jnp.transpose(h_init[0], (1, 2, 0))
         c_in = jnp.transpose(c_init[0], (1, 2, 0))
         stack = pltpu.VMEM((tiles + 1, 3 * ch, height), jnp.bfloat16)
-        hbm_spec = pl.BlockSpec(memory_space=pltpu.MemorySpace.HBM)
         vmem_spec = pl.BlockSpec(memory_space=pltpu.VMEM)
         dma = pltpu.SemaphoreType.DMA
         h_seq, c_last = pl.pallas_call(
             functools.partial(kernel, steps, tiles, rows_n, cols_n),
             out_shape=(jax.ShapeDtypeStruct((steps, width, ch, height), jnp.bfloat16),
                        jax.ShapeDtypeStruct((width, ch, height), jnp.float32)),
-            in_specs=[hbm_spec, hbm_spec, vmem_spec, hbm_spec],
+            in_specs=[vmem_spec] * 4,
             out_specs=(vmem_spec, vmem_spec),
             scratch_shapes=[
                 stack, stack, stack, stack,
                 pltpu.VMEM((gates_n, 9 * ch), jnp.bfloat16),
-                pltpu.VMEM((steps, gates_n), jnp.float32),
                 pltpu.VMEM((gates_n, height), jnp.float32),
                 pltpu.VMEM((ch, height), jnp.float32),
                 pltpu.VMEM((ch, height), jnp.bfloat16),
@@ -280,7 +269,7 @@
                 pltpu.VMEM((2, 2, ch, height), jnp.bfloat16),
                 pltpu.VMEM((2, 2, ch, height), jnp.bfloat16),
                 pltpu.VMEM((2, 4, 16, height), jnp.bfloat16),
-                dma((2 + width,)), dma((2, 2)), dma((2, 2)), dma((2, 2)), dma((2, 2)), dma((2, 4)), dma((2, 4)),
+                dma((2, 2)), dma((2, 2)), dma((2, 2)), dma((2, 2)), dma((2, 4)), dma((2, 4)),
             ],
             compiler_params=pltpu.CompilerParams(collective_id=0, has_side_effects=True, vmem_limit_bytes=32 * 1024 * 1024),
         )(h_in, c_in, w, gate_bias)

time: 137 us -> 136 us (level)
  no operation moved by 1% of the time
where the time goes in v7:
time: 136 us
  Pallas kernels  124 us (91%)
  local copies, waits for them, and re-layouts  11.3 us (8%)
    pallas_call x1, Pallas kernels, device_fn(): pl.pallas_call(functools.partial(kernel, steps, tiles, rows_n, cols_n), o...  124 us
    unnamed x9, local copies, waits for them, and re-layouts  11.1 us

profile of v7, /device:TPU:0, one launch (start us, length us, event | category | flops | bytes accessed | tf_op | source)
XLA Modules:
  0.0 136.0 jit_solution(4700740525203982683)
XLA Ops:
  0.6 1.0 copy.8
  1.6 0.2 copy.9.w_ref
  1.8 0.0 copy-start
  1.8 1.2 copy-done
  3.0 0.0 copy-start.1
  3.0 1.0 copy-done.1
  4.1 0.0 copy-start.2
  4.1 0.8 copy-done.2
  4.8 124.0 %shard_map.59 = (bf16[32,32,64,128]{3,2,1,0:T(8,128)(2,1)S(1)}, f32[32,64,128]{2,1,0:T(8,128)S(1)}) custom-call(bf16[32,64,128]{2,1,0:T(8,128)(2,1)S(1)} %bitcast.20, f32[32,64,128]{2,1,0:T(8,128)S(1)} %bitcast.19, bf16[256,576]{1,0:T(8,128)(2,1)S(1)} %copy.9.w_ref, f32[32,256]{1,0:T(8,128)S(1)} %copy-done.2), custom_call_target="tpu_custom_call" | custom-call | tf_op jit(solution)/shard_map/pallas_call | solution.py:255
  128.9 6.2 %copy.13 = bf16[32,1,128,32,64]{2,4,3,1,0:T(8,128)(2,1)} copy(bf16[32,1,128,32,64]{2,4,3,1,0:T(8,128)(2,1)S(1)} %bitcast.17) | data formatting | bytes 33554432
  135.0 1.0 copy.14
Async XLA Ops:
  1.8 1.2 copy-start
  3.0 1.0 copy-start.1
  4.1 0.8 copy-start.2

commit v8 on v7

--- a/solution.py
+++ b/solution.py
@@ -88,6 +88,8 @@
     def send_strip_to(p, live=None):
         for d in DIAGONALS:
             at(d, lambda d=d: diag_copy(p, d).start(), live)
+
+    def send_strip_rows(p, live=None):
         for d in (UP, DOWN):
             at(d, lambda d=d: strip_copy(p, d).start(), live)
 
@@ -198,6 +200,7 @@
             gates = following
             if j == 0:
                 send_cols(q, live)
+                send_strip_rows(q, live)
                 gates = matmul(p, 1)
         for g in groups:
             inner[pl.ds(16 * g, 16)] = packed[g]
@@ -224,6 +227,7 @@
     store_strip(0, jnp.concatenate([jnp.where(even, e, roll(e, -2)) for e in edge], axis=0))
     send_strip_to(0)
     send_cols(0)
+    send_strip_rows(0)
 
     def two_steps(i, carry):
         step(2 * i, 0)

time: 136 us -> 136 us (level)
  no operation moved by 1% of the time
where the time goes in v8:
time: 136 us
  Pallas kernels  124 us (91%)
  local copies, waits for them, and re-layouts  11.3 us (8%)
    pallas_call x1, Pallas kernels, device_fn(): pl.pallas_call(functools.partial(kernel, steps, tiles, rows_n, cols_n), o...  124 us
    unnamed x9, local copies, waits for them, and re-layouts  11.1 us

profile of v8, /device:TPU:0, one launch (start us, length us, event | category | flops | bytes accessed | tf_op | source)
XLA Modules:
  0.0 135.7 jit_solution(3476743655665079676)
XLA Ops:
  0.6 1.0 copy.8
  1.6 0.2 copy.9.w_ref
  1.8 0.0 copy-start
  1.8 1.2 copy-done
  3.0 0.0 copy-start.1
  3.0 1.0 copy-done.1
  4.1 0.0 copy-start.2
  4.1 0.8 copy-done.2
  4.8 123.7 %shard_map.59 = (bf16[32,32,64,128]{3,2,1,0:T(8,128)(2,1)S(1)}, f32[32,64,128]{2,1,0:T(8,128)S(1)}) custom-call(bf16[32,64,128]{2,1,0:T(8,128)(2,1)S(1)} %bitcast.20, f32[32,64,128]{2,1,0:T(8,128)S(1)} %bitcast.19, bf16[256,576]{1,0:T(8,128)(2,1)S(1)} %copy.9.w_ref, f32[32,256]{1,0:T(8,128)S(1)} %copy-done.2), custom_call_target="tpu_custom_call" | custom-call | tf_op jit(solution)/shard_map/pallas_call | solution.py:259
  128.6 6.2 %copy.13 = bf16[32,1,128,32,64]{2,4,3,1,0:T(8,128)(2,1)} copy(bf16[32,1,128,32,64]{2,4,3,1,0:T(8,128)(2,1)S(1)} %bitcast.17) | data formatting | bytes 33554432
  134.8 1.0 copy.14
Async XLA Ops:
  1.8 1.2 copy-start
  3.0 1.0 copy-start.1
  4.1 0.8 copy-start.2
